TPU v7x, 32 devices: a whole 2x2x4 slice. The times are simulated.
32 devices in a mesh: dp: 2 (over core), seq: 16 (over z, y, x).
Axes of the slice: x: 2, y: 2, z: 4, core: 2. Of those that a mesh axis runs over, the one named last changes fastest.
Arguments:
- latent: bfloat16 [32, 1024, 1152], P(('dp', 'seq')), parts along dimension 0, may hold values from -6 to 6
- w_qkv_space: bfloat16 [1152, 1728], replicated, may hold values from -0.1875 to 0.1875
- w_out_space: bfloat16 [576, 1152], replicated, may hold values from -0.25 to 0.25
- w_qkv_time: bfloat16 [1152, 1728], replicated, may hold values from -0.1875 to 0.1875
- w_out_time: bfloat16 [576, 1152], replicated, may hold values from -0.25 to 0.25
- modulation: float32 [12, 1152], P('dp'), parts along dimension 0, may hold values from -1.5 to 5
Outputs:
- block_out: bfloat16 [32, 1024, 1152], P(('dp', 'seq')), parts along dimension 0
There are 2 independent parts, one for each index of `dp`. A program takes and returns all parts, laid end to end along the dimension named above; an argument that names none is the same for every part. Nothing has to cross between parts.
All inputs are finite; a program needn't handle non-finite values.
Results may differ from a plain program's by a relative error of at most 0.02.
The roundings to bfloat16 on the way count: a program that leaves them out, or rounds other values in their place, can miss the bound.
Values may be sent and summed in bfloat16 or wider, within the bound.
No kernel may reach another device: no remote copies, remote signals or barrier semaphores. Data moves between devices by JAX's collectives and lax.ppermute only.
A program may use at most 128 MiB of HBM per device.

v0:
```python
import jax
import jax.numpy as jnp
from jax import lax
from jax.sharding import PartitionSpec as P

HEADS = 8
HEAD_DIM = 72
EPS = 1e-06


def normalize(values):
    center = jnp.mean(values, -1, keepdims=True)
    centred = values - center
    spread = jnp.mean(centred * centred, -1, keepdims=True)
    return centred * lax.rsqrt(spread + EPS)


def modulated(latent, modulation, first):
    normed = normalize(latent.astype(jnp.float32))
    return (normed * (1.0 + modulation[first + 1]) + modulation[first]).astype(jnp.bfloat16)


def softmax_weights(scores, axis):
    top_score = jnp.max(scores, axis, keepdims=True)
    expo = jnp.exp(scores - top_score)
    return (expo / jnp.sum(expo, axis, keepdims=True)).astype(jnp.bfloat16)


def attend_space(frame_rows, w_qkv, w_out, modulation):
    tokens_here = frame_rows.shape[0]
    mixed = modulated(frame_rows, modulation, 0)
    triple = jnp.dot(mixed, w_qkv, preferred_element_type=jnp.float32).astype(jnp.bfloat16)
    triple = triple.reshape(tokens_here, 3, HEADS, HEAD_DIM)
    factor = 1.0 / float(HEAD_DIM) ** 0.5
    scores = (
        jnp.einsum("shd,thd->hst", triple[:, 0], triple[:, 1], preferred_element_type=jnp.float32)
        * factor
    )
    weights = softmax_weights(scores, 2)
    outputs = jnp.einsum(
        "hst,thd->shd", weights, triple[:, 2], preferred_element_type=jnp.float32
    ).astype(jnp.bfloat16)
    delta = jnp.dot(
        outputs.reshape(tokens_here, HEADS * HEAD_DIM), w_out, preferred_element_type=jnp.float32
    )
    return (frame_rows.astype(jnp.float32) + modulation[2] * delta).astype(jnp.bfloat16)


def attend_time(queries, key_heads, value_heads):
    factor = 1.0 / float(queries.shape[-1]) ** 0.5
    scores = (
        jnp.einsum("fphd,gphd->phfg", queries, key_heads, preferred_element_type=jnp.float32)
        * factor
    )
    weights = softmax_weights(scores, 3)
    return jnp.einsum(
        "phfg,gphd->fphd", weights, value_heads, preferred_element_type=jnp.float32
    ).astype(jnp.bfloat16)


def shards(latent, w_qkv_space, w_out_space, w_qkv_time, w_out_time, modulation):
    after_space = attend_space(latent[0], w_qkv_space, w_out_space, modulation)
    spatial, width = after_space.shape
    patches = lax.all_to_all(after_space[None], "seq", split_axis=1, concat_axis=0, tiled=True)
    frames, positions, width = patches.shape
    mixed = modulated(patches, modulation, 3).reshape(frames * positions, width)
    triple = jnp.dot(mixed, w_qkv_time, preferred_element_type=jnp.float32).astype(jnp.bfloat16)
    triple = triple.reshape(frames, positions, 3, HEADS, HEAD_DIM)
    outputs = attend_time(triple[:, :, 0], triple[:, :, 1], triple[:, :, 2])
    delta = jnp.dot(
        outputs.reshape(frames * positions, HEADS * HEAD_DIM),
        w_out_time,
        preferred_element_type=jnp.float32,
    )
    result = patches.astype(jnp.float32).reshape(frames * positions, width) + modulation[5] * delta
    result = result.astype(jnp.bfloat16).reshape(frames, positions, width)
    return lax.all_to_all(result, "seq", split_axis=0, concat_axis=1, tiled=True)


def solution(mesh):
    in_specs = (P(("dp", "seq"), None, None), P(), P(), P(), P(), P("dp", None))
    out_specs = P(("dp", "seq"), None, None)
    return jax.shard_map(shards, mesh=mesh, in_specs=in_specs, out_specs=out_specs, check_vma=False)
```

profile of v0, /device:TPU:0, one launch (start us, length us, event | category | flops | bytes accessed | tf_op | source)
XLA Modules:
  0.0 269.0 jit_solution(783976993422969830)
XLA Ops:
  0.0 0.0 copy-start
  0.0 0.0 copy-start.2
  0.0 1.2 slice_reduce_fusion.1
  1.2 2.1 convert_reduce_fusion.1
  3.3 0.0 copy-done.2
  3.3 0.8 fusion.13
  4.0 9.2 %convolution_convert_fusion.1 = bf16[1024,1728]{0,1:T(8,128)(2,1)} fusion(bf16[1152,1728]{0,1:T(8,128)(2,1)} %param.7, bf16[1,1024,1152]{2,1,0:T(8,128)(2,1)S(1)} %copy-done.2, f32[1152]{0:T(1024)S(1)} %get-tuple-element.6, f32[1152]{0:T(1024)S(1)} %get-tuple-element.7, f32[1024]{0:T(1024)S(1)} %add_rsqrt_fusion.1, f32[1024]{0:T(1024)S(1)} %broadcast_multiply_fusion.1), kind=kOutput, calls=%fused_computation.36 | convolution fusion | flops 4085710848 | bytes 9896960 | tf_op jit(solution)/shard_map/dot_general | solution.py:32
  13.2 17.8 %fusion.55 = (f32[8,1024]{1,0:T(8,128)S(1)}, f32[8,1024,1024]{1,2,0:T(8,128)}) fusion(bf16[1024,3,8,72]{0,3,2,1:T(8,128)(2,1)} %bitcast.104), kind=kOutput, calls=%fused_computation.75 | convolution fusion | flops 1233126400 | bytes 35946496 | tf_op jit(solution)/shard_map/sub | solution.py:25
  31.0 0.0 copy-start.3
  31.1 12.8 %fusion.50 = bf16[8,72,1024]{2,1,0:T(8,128)(2,1)S(1)} fusion(f32[8,1024,1024]{1,2,0:T(8,128)} %get-tuple-element.17, f32[8,1024]{1,0:T(8,128)S(1)} %get-tuple-element.16, bf16[1024,3,8,72]{0,3,2,1:T(8,128)(2,1)} %bitcast.105), kind=kOutput, calls=%fused_computation.57 | convolution fusion | flops 1225326592 | bytes 35946496 | tf_op jit(solution)/shard_map/hst,thd->shd/dot_general | solution.py:40
  43.9 0.0 copy-done
  43.9 0.0 copy-done.3
  43.9 2.4 fusion.26
  46.3 5.8 %copy.37 = bf16[1,1024,1152]{2,0,1:T(2,128)(2,1)} copy(bf16[1,1024,1152]{2,1,0:T(8,128)(2,1)S(1)} %fusion.26) | data formatting | bytes 4718592 | tf_op jit(solution)/shard_map/broadcast_in_dim | solution.py:64
  52.1 0.5 broadcast.73
  52.6 16.3 %reduce.15 = bf16[1024,1152]{1,0:T(8,128)(2,1)} reduce(bf16[1024,1,1152]{2,1,0:T(2,128)(2,1)} %bitcast.100, bf16[]{:T(256)} %broadcast.73), dimensions={1}, to_apply=%bitcast.99.reduce_sub_computation | reduce | bytes 4718594
  68.9 4.1 %reshape.90 = bf16[16,2,36864]{2,1,0:T(2,128)(2,1)} reshape(bf16[1024,1152]{1,0:T(8,128)(2,1)} %reduce.15) | data formatting | bytes 4718592
  73.0 63.4 %all_to_all.21 = bf16[16,2,36864]{2,1,0:T(2,128)(2,1)} all-to-all(bf16[16,2,36864]{2,1,0:T(2,128)(2,1)} %reshape.90), channel_id=1, replica_groups=mesh['dp'=2,'seq'=16] {'seq'}, dimensions={0} | all-to-all | bytes 4718592 | tf_op jit(solution)/shard_map/all_to_all | solution.py:64
  136.4 10.7 %reshape.91 = bf16[1024,1,1152]{2,1,0:T(2,128)(2,1)} reshape(bf16[16,2,36864]{2,1,0:T(2,128)(2,1)} %all_to_all.21) | data formatting | bytes 4718592
  147.1 0.0 copy-start.4
  147.1 2.9 %convert_reduce_fusion = (f32[1024]{0:T(1024)S(1)}, bf16[1,1024,1152]{2,1,0:T(8,128)(2,1)S(1)}) fusion(bf16[1,1024,1152]{2,0,1:T(2,128)(2,1)} %bitcast.101), kind=kLoop, calls=%fused_computation.9 | loop fusion | flops 2358272 | bytes 4722688 | tf_op jit(solution)/shard_map/reduce_sum | solution.py:12
  150.0 0.0 copy-start.1
  150.1 0.8 fusion.24
  150.8 0.6 copy-done.1
  151.5 0.0 copy-done.4
  151.5 7.1 %convolution_convert_fusion = bf16[1024,1728]{0,1:T(8,128)(2,1)} fusion(bf16[1152,1728]{0,1:T(8,128)(2,1)S(1)} %copy-done.4, bf16[1,1024,1152]{2,1,0:T(8,128)(2,1)S(1)} %get-tuple-element.12, f32[1152]{0:T(1024)S(1)} %get-tuple-element.9, f32[1152]{0:T(1024)S(1)} %get-tuple-element.10, f32[1024]{0:T(1024)S(1)} %add_rsqrt_fusion, ...), kind=kOutput, calls=%fused_computation.35 | convolution fusion | flops 4085710848 | bytes 9896960 | tf_op jit(solution)/shard_map/dot_general | solution.py:67
  158.6 9.9 %reshape.83 = bf16[16,64,3,8,72]{1,0,4,3,2:T(8,128)(2,1)} reshape(bf16[1024,1728]{0,1:T(8,128)(2,1)} %convolution_convert_fusion) | data formatting | bytes 7077888 | tf_op jit(solution)/shard_map/reshape | solution.py:68
  168.5 6.7 %fusion.54 = (bf16[16,64,1,8,72]{1,0,4,3,2:T(8,128)(2,1)}, bf16[16,64,1,8,72]{1,0,4,3,2:T(8,128)(2,1)}, bf16[16,64,1,8,72]{1,0,4,3,2:T(8,128)(2,1)}) fusion(bf16[16,64,3,8,72]{1,0,4,3,2:T(8,128)(2,1)} %reshape.83), kind=kLoop, calls=%fused_computation.74 | loop fusion | bytes 7077888 | tf_op jit(solution)/shard_map/slice | solution.py:69
  175.3 5.4 %copy.33 = bf16[16,64,1,8,72]{4,0,3,1,2:T(8,128)(2,1)S(1)} copy(bf16[16,64,1,8,72]{1,0,4,3,2:T(8,128)(2,1)} %get-tuple-element.14) | data formatting | bytes 2359296
  180.6 6.3 %copy.34 = bf16[16,64,1,8,72]{4,0,3,1,2:T(8,128)(2,1)} copy(bf16[16,64,1,8,72]{1,0,4,3,2:T(8,128)(2,1)} %get-tuple-element.15) | data formatting | bytes 2359296
  186.9 2.8 %fusion.42 = f32[64,8,16,16]{2,3,1,0:T(8,128)S(1)} fusion(bf16[16,64,1,8,72]{4,0,3,1,2:T(8,128)(2,1)} %copy.34, bf16[16,64,1,8,72]{4,0,3,1,2:T(8,128)(2,1)S(1)} %copy.33), kind=kOutput, calls=%fused_computation.50 | convolution fusion | flops 18874368 | bytes 2883584 | tf_op jit(solution)/shard_map/fphd,gphd->phfg/dot_general | solution.py:52
  189.7 4.2 %fusion.56 = (f32[64,8,16]{2,1,0:T(8,128)}, f32[64,8,16,16]{2,3,1,0:T(8,128)}) fusion(f32[64,8,16,16]{2,3,1,0:T(8,128)S(1)} %fusion.42), kind=kOutput, calls=%fused_computation.76 | output fusion | flops 524303 | bytes 1081344 | tf_op jit(solution)/shard_map/sub | solution.py:25
  193.9 5.4 %copy.32 = bf16[16,64,1,8,72]{4,0,3,1,2:T(8,128)(2,1)S(1)} copy(bf16[16,64,1,8,72]{1,0,4,3,2:T(8,128)(2,1)} %get-tuple-element.13) | data formatting | bytes 2359296
  199.3 3.1 %convert_bitcast_fusion.2 = bf16[16,64,8,72]{3,0,2,1:T(8,128)(2,1)S(1)} fusion(f32[64,8,16,16]{2,3,1,0:T(8,128)} %get-tuple-element.19, f32[64,8,16]{2,1,0:T(8,128)} %get-tuple-element.18, bf16[16,64,1,8,72]{4,0,3,1,2:T(8,128)(2,1)S(1)} %copy.32), kind=kOutput, calls=%fused_computation.54 | convolution fusion | flops 19726336 | bytes 2916352 | tf_op jit(solution)/shard_map/phfg,gphd->fphd/dot_general | solution.py:56
  202.3 0.5 copy.27
  202.9 2.5 reshape.80
  205.4 4.6 %fusion.22 = bf16[1024,1152]{1,0:T(8,128)(2,1)S(1)} fusion(bf16[1,1024,1152]{2,1,0:T(8,128)(2,1)} %copy-done.1, bf16[1024,576]{1,0:T(8,128)(2,1)} %reshape.80, bf16[576,1152]{1,0:T(8,128)(2,1)} %param.10, f32[1152]{0:T(1024)S(1)} %get-tuple-element.5), kind=kOutput, calls=%fused_computation.30 | convolution fusion | flops 1363673088 | bytes 7229952 | tf_op jit(solution)/shard_map/dot_general | solution.py:70
  210.0 57.6 %all_to_all.22 = bf16[16,64,1152]{2,1,0:T(8,128)(2,1)S(1)} all-to-all(bf16[16,64,1152]{2,1,0:T(8,128)(2,1)S(1)} %bitcast.103), channel_id=1, replica_groups=mesh['dp'=2,'seq'=16] {'seq'}, dimensions={0} | all-to-all | bytes 4718592 | tf_op jit(solution)/shard_map/all_to_all | solution.py:77
  267.6 1.4 copy.39
  (4 shorter events, 0.0 us)
Async XLA Ops:
  0.0 43.9 %copy-start = (bf16[576,1152]{1,0:T(8,128)(2,1)S(1)}, bf16[576,1152]{1,0:T(8,128)(2,1)}, u32[]{:S(2)}) copy-start(bf16[576,1152]{1,0:T(8,128)(2,1)} %param.8) | copy-start | bytes 3981316
  0.0 3.3 %copy-start.2 = (bf16[1,1024,1152]{2,1,0:T(8,128)(2,1)S(1)}, bf16[1,1024,1152]{2,1,0:T(8,128)(2,1)}, u32[]{:S(2)}) copy-start(bf16[1,1024,1152]{2,1,0:T(8,128)(2,1)} %param.6) | copy-start | bytes 7077892
  31.0 12.9 %copy-start.3 = (bf16[1,1024,1152]{2,1,0:T(8,128)(2,1)S(1)}, bf16[1,1024,1152]{2,1,0:T(8,128)(2,1)}, u32[]{:S(2)}) copy-start(bf16[1,1024,1152]{2,1,0:T(8,128)(2,1)} %param.6) | copy-start | bytes 7077892
  147.1 4.3 %copy-start.4 = (bf16[1152,1728]{0,1:T(8,128)(2,1)S(1)}, bf16[1152,1728]{0,1:T(8,128)(2,1)}, u32[]{:S(2)}) copy-start(bf16[1152,1728]{0,1:T(8,128)(2,1)} %param.9) | copy-start | bytes 11943940
  150.0 1.4 copy-start.1
where the time goes:
time: 270 us; the launch traced here: 269 us
  blocking collectives  121 us (45%)
  local copies, waits for them, and re-layouts  59.8 us (22%)
  matrix products  59.8 us (22%)
  other arithmetic  28.2 us (10%)
    all_to_all x1, blocking collectives, shards(): lax.all_to_all(after_space[None], 'seq', split_axis=1, concat_axis=0, til...  63.4 us
    all_to_all x1, blocking collectives, shards(): lax.all_to_all(result, 'seq', split_axis=0, concat_axis=1, tiled=True)  57.6 us
    unnamed x17, local copies, waits for them, and re-layouts  34.3 us
    sub x1, matrix products, softmax_weights(): expo = jnp.exp(scores - top_score)  17.8 us
    unnamed x1, other arithmetic  16.3 us
    dot_general x1, matrix products, attend_space(): jnp.einsum('hst,thd->shd', weights, triple[:, 2], preferred_element_type=...  12.8 us
    reshape x1, local copies, waits for them, and re-layouts, shards(): triple = triple.reshape(frames, positions, 3, HEADS, HEAD_DIM)  9.93 us
    dot_general x1, matrix products, attend_space(): jnp.dot(mixed, w_qkv, preferred_element_type=jnp.float32)  9.17 us

commit v1 on v0

--- a/solution.py
+++ b/solution.py
@@ -61,7 +61,12 @@
 def shards(latent, w_qkv_space, w_out_space, w_qkv_time, w_out_time, modulation):
     after_space = attend_space(latent[0], w_qkv_space, w_out_space, modulation)
     spatial, width = after_space.shape
-    patches = lax.all_to_all(after_space[None], "seq", split_axis=1, concat_axis=0, tiled=True)
+    patches = jnp.concatenate(
+        lax.all_to_all(
+            jnp.stack(jnp.split(after_space[None], lax.axis_size("seq"), axis=1)), "seq", 0, 0
+        ),
+        axis=0,
+    )
     frames, positions, width = patches.shape
     mixed = modulated(patches, modulation, 3).reshape(frames * positions, width)
     triple = jnp.dot(mixed, w_qkv_time, preferred_element_type=jnp.float32).astype(jnp.bfloat16)

time: 270 us -> 244 us (0.904)
  local copies, waits for them, and re-layouts: 59.8 us -> 41.3 us
  other arithmetic: 28.2 us -> 24.7 us
  matrix products: 59.8 us -> 56.7 us
    unnamed x1 -> x0, other arithmetic: 16.3 us -> none
    unnamed x17 -> x33, local copies, waits for them, and re-layouts: 34.3 us -> 21.4 us
    sub x1, other arithmetic: 4.17 us -> 16.1 us  [softmax_weights(): expo = jnp.exp(scores - top_score)]
    broadcast_in_dim x1 -> x0, local copies, waits for them, and re-layouts: 5.76 us -> none  [shards(): after_space[None]]
    convert_element_type x0 -> x1, other arithmetic: none -> 2.75 us  [modulated(): (normed * (1.0 + modulation[first + 1]) + modulation[first]).astype(jnp.b...]
where the time goes in v1:
time: 244 us
  blocking collectives  121 us (50%)
  matrix products  56.7 us (23%)
  local copies, waits for them, and re-layouts  41.3 us (17%)
  other arithmetic  24.7 us (10%)
    all_to_all x1, blocking collectives, shards(): lax.all_to_all(jnp.stack(jnp.split(after_space[None], lax.axis_size('seq'...  63.1 us
    all_to_all x1, blocking collectives, shards(): lax.all_to_all(result, 'seq', split_axis=0, concat_axis=1, tiled=True)  57.6 us
    unnamed x33, local copies, waits for them, and re-layouts  21.4 us
    sub x1, matrix products, softmax_weights(): expo = jnp.exp(scores - top_score)  17.8 us
    sub x1, other arithmetic, softmax_weights(): expo = jnp.exp(scores - top_score)  16.1 us
    dot_general x1, matrix products, attend_space(): jnp.einsum('hst,thd->shd', weights, triple[:, 2], preferred_element_type=...  12.7 us
    reshape x1, local copies, waits for them, and re-layouts, shards(): triple = triple.reshape(frames, positions, 3, HEADS, HEAD_DIM)  9.93 us
    dot_general x1, matrix products, attend_space(): jnp.dot(mixed, w_qkv, preferred_element_type=jnp.float32)  9.16 us

profile of v1, /device:TPU:0, one launch (start us, length us, event | category | flops | bytes accessed | tf_op | source)
XLA Modules:
  0.0 243.7 jit_solution(10484469426005071835)
XLA Ops:
  0.0 0.0 copy-start
  0.0 0.0 copy-start.2
  0.0 0.0 copy-start.5
  0.0 2.2 convert_reduce_fusion
  2.2 0.3 copy-done.2
  2.5 0.8 fusion.11
  3.3 0.0 copy-done.5
  3.3 0.1 slice_reduce_fusion.1
  3.4 9.2 %convolution_convert_fusion.1 = bf16[1024,1728]{0,1:T(8,128)(2,1)} fusion(bf16[1152,1728]{0,1:T(8,128)(2,1)} %param.7, bf16[1,1024,1152]{2,1,0:T(8,128)(2,1)S(1)} %copy-done.2, f32[1152]{0:T(1024)S(1)} %get-tuple-element.6, f32[1152]{0:T(1024)S(1)} %get-tuple-element.7, f32[1024]{0:T(1024)S(1)} %add_rsqrt_fusion.1, f32[1024]{0:T(1024)S(1)} %broadcast_multiply_fusion.1), kind=kOutput, calls=%fused_computation.35 | convolution fusion | flops 4085710848 | bytes 9896960 | tf_op jit(solution)/shard_map/dot_general | solution.py:32
  12.5 17.8 %fusion.64 = (f32[8,1024]{1,0:T(8,128)S(1)}, f32[8,1024,1024]{1,2,0:T(8,128)}) fusion(bf16[1024,3,8,72]{0,3,2,1:T(8,128)(2,1)} %bitcast.165), kind=kOutput, calls=%fused_computation.102 | convolution fusion | flops 1233126400 | bytes 35946496 | tf_op jit(solution)/shard_map/sub | solution.py:25
  30.4 0.0 copy-start.3
  30.4 12.7 %fusion.43 = bf16[8,72,1024]{2,1,0:T(8,128)(2,1)S(1)} fusion(f32[8,1024,1024]{1,2,0:T(8,128)} %get-tuple-element.15, f32[8,1024]{1,0:T(8,128)S(1)} %get-tuple-element.14, bf16[1024,3,8,72]{0,3,2,1:T(8,128)(2,1)} %bitcast.166), kind=kOutput, calls=%fused_computation.52 | convolution fusion | flops 1225326592 | bytes 35946496 | tf_op jit(solution)/shard_map/hst,thd->shd/dot_general | solution.py:40
  43.0 0.0 copy-done
  43.0 0.0 copy-done.3
  43.0 2.4 fusion.24
  45.8 63.1 %all_to_all.17 = bf16[16,1,64,1152]{3,2,1,0:T(8,128)(2,1)S(1)} all-to-all(bf16[16,1,64,1152]{3,2,1,0:T(8,128)(2,1)S(1)} %fusion.45), channel_id=1, replica_groups=mesh['dp'=2,'seq'=16] {'seq'}, dimensions={0} | all-to-all | bytes 4718592 | tf_op jit(solution)/shard_map/all_to_all | solution.py:65
  108.9 0.0 copy-start.1
  108.9 1.4 copy-done.1
  110.3 0.4 convert_reduce_fusion.1
  110.7 0.1 div.35
  110.8 2.4 fusion.17
  113.2 0.1 rsqrt.21
  113.3 0.0 copy-start.6
  113.3 2.7 %fusion.21 = bf16[1024,1152]{1,0:T(8,128)(2,1)S(1)} fusion(bf16[16,1,64,1152]{3,2,1,0:T(8,128)(2,1)} %copy-done.1, f32[1152]{0:T(1024)S(1)} %get-tuple-element.9, f32[1152]{0:T(1024)S(1)} %get-tuple-element.10, f32[1024]{0:T(1024)S(1)} %rsqrt.21, f32[1024]{0:T(1024)S(1)} %div.35), kind=kLoop, calls=%fused_computation.30 | loop fusion | flops 7077888 | bytes 4736000 | tf_op jit(solution)/shard_map/convert_element_type | solution.py:20
  116.1 0.1 copy-done.6
  116.2 6.2 %convolution_convert_fusion = bf16[1024,1728]{0,1:T(8,128)(2,1)} fusion(bf16[1024,1152]{1,0:T(8,128)(2,1)S(1)} %fusion.21, bf16[1152,1728]{0,1:T(8,128)(2,1)S(1)} %copy-done.6), kind=kOutput, calls=%fused_computation.34 | convolution fusion | flops 4078632960 | bytes 9879552 | tf_op jit(solution)/shard_map/dot_general | solution.py:72
  122.4 9.9 %reshape.82 = bf16[16,64,3,8,72]{1,0,4,3,2:T(8,128)(2,1)} reshape(bf16[1024,1728]{0,1:T(8,128)(2,1)} %convolution_convert_fusion) | data formatting | bytes 7077888 | tf_op jit(solution)/shard_map/reshape | solution.py:73
  132.3 6.7 %fusion.63 = (bf16[16,64,1,8,72]{1,0,4,3,2:T(8,128)(2,1)}, bf16[16,64,1,8,72]{1,0,4,3,2:T(8,128)(2,1)}, bf16[16,64,1,8,72]{1,0,4,3,2:T(8,128)(2,1)}) fusion(bf16[16,64,3,8,72]{1,0,4,3,2:T(8,128)(2,1)} %reshape.82), kind=kLoop, calls=%fused_computation.101 | loop fusion | bytes 7077888 | tf_op jit(solution)/shard_map/slice | solution.py:74
  139.0 6.3 %copy.23 = bf16[16,64,1,8,72]{4,0,3,1,2:T(8,128)(2,1)} copy(bf16[16,64,1,8,72]{1,0,4,3,2:T(8,128)(2,1)} %get-tuple-element.11) | data formatting | bytes 2359296
  145.3 5.4 %copy.24 = bf16[16,64,1,8,72]{4,0,3,1,2:T(8,128)(2,1)S(1)} copy(bf16[16,64,1,8,72]{1,0,4,3,2:T(8,128)(2,1)} %get-tuple-element.12) | data formatting | bytes 2359296
  150.7 6.3 %copy.25 = bf16[16,64,1,8,72]{4,0,3,1,2:T(8,128)(2,1)} copy(bf16[16,64,1,8,72]{1,0,4,3,2:T(8,128)(2,1)} %get-tuple-element.13) | data formatting | bytes 2359296
  156.9 2.8 %fusion.35 = f32[64,8,16,16]{2,3,1,0:T(8,128)S(1)} fusion(bf16[16,64,1,8,72]{4,0,3,1,2:T(8,128)(2,1)} %copy.25, bf16[16,64,1,8,72]{4,0,3,1,2:T(8,128)(2,1)S(1)} %copy.24), kind=kOutput, calls=%fused_computation.45 | convolution fusion | flops 18874368 | bytes 2883584 | tf_op jit(solution)/shard_map/fphd,gphd->phfg/dot_general | solution.py:52
  159.8 0.0 copy-start.4
  159.8 16.1 %fusion.65 = (f32[64,8,16]{2,1,0:T(8,128)S(1)}, f32[64,8,16,16]{2,3,1,0:T(8,128)S(1)}) fusion(f32[64,8,16,16]{2,3,1,0:T(8,128)S(1)} %fusion.35), kind=kOutput, calls=%fused_computation.103 | output fusion | flops 524303 | bytes 1081344 | tf_op jit(solution)/shard_map/sub | solution.py:25
  175.8 0.0 copy-done.4
  175.8 1.1 convert_bitcast_fusion.1
  176.9 0.5 copy.18
  177.5 2.5 %reshape.79 = bf16[1024,576]{1,0:T(8,128)(2,1)} reshape(bf16[16,64,8,72]{3,2,1,0:T(8,128)(2,1)S(1)} %copy.18) | data formatting | bytes 2359296 | tf_op jit(solution)/shard_map/reshape | solution.py:76
  180.0 4.6 %fusion.22 = bf16[1024,1152]{1,0:T(8,128)(2,1)S(1)} fusion(bf16[16,1,64,1152]{3,2,1,0:T(8,128)(2,1)} %copy-done.1, bf16[1024,576]{1,0:T(8,128)(2,1)} %reshape.79, bf16[576,1152]{1,0:T(8,128)(2,1)} %param.10, f32[1152]{0:T(1024)S(1)} %get-tuple-element.5), kind=kOutput, calls=%fused_computation.31 | convolution fusion | flops 1363673088 | bytes 7229952 | tf_op jit(solution)/shard_map/dot_general | solution.py:75
  184.6 57.6 %all_to_all.18 = bf16[16,64,1152]{2,1,0:T(8,128)(2,1)S(1)} all-to-all(bf16[16,64,1152]{2,1,0:T(8,128)(2,1)S(1)} %bitcast.164), channel_id=1, replica_groups=mesh['dp'=2,'seq'=16] {'seq'}, dimensions={0} | all-to-all | bytes 4718592 | tf_op jit(solution)/shard_map/all_to_all | solution.py:82
  242.2 1.4 copy.42
  (20 shorter events, 0.3 us)
Async XLA Ops:
  0.0 43.0 %copy-start = (bf16[576,1152]{1,0:T(8,128)(2,1)S(1)}, bf16[576,1152]{1,0:T(8,128)(2,1)}, u32[]{:S(2)}) copy-start(bf16[576,1152]{1,0:T(8,128)(2,1)} %param.8) | copy-start | bytes 3981316
  0.0 2.5 %copy-start.2 = (bf16[1,1024,1152]{2,1,0:T(8,128)(2,1)S(1)}, bf16[1,1024,1152]{2,1,0:T(8,128)(2,1)}, u32[]{:S(2)}) copy-start(bf16[1,1024,1152]{2,1,0:T(8,128)(2,1)} %param.6) | copy-start | bytes 7077892
  0.0 3.3 %copy-start.5 = (f32[6,1152]{1,0:T(8,128)S(1)}, f32[6,1152]{1,0:T(8,128)}, u32[]{:S(2)}) copy-start(f32[6,1152]{1,0:T(8,128)} %param.11) | copy-start | bytes 82948
  30.4 12.7 %copy-start.3 = (bf16[1,1024,1152]{2,1,0:T(8,128)(2,1)S(1)}, bf16[1,1024,1152]{2,1,0:T(8,128)(2,1)}, u32[]{:S(2)}) copy-start(bf16[1,1024,1152]{2,1,0:T(8,128)(2,1)} %param.6) | copy-start | bytes 7077892
  108.9 1.4 copy-start.1
  113.3 2.8 %copy-start.6 = (bf16[1152,1728]{0,1:T(8,128)(2,1)S(1)}, bf16[1152,1728]{0,1:T(8,128)(2,1)}, u32[]{:S(2)}) copy-start(bf16[1152,1728]{0,1:T(8,128)(2,1)} %param.9) | copy-start | bytes 11943940
  159.8 16.1 %copy-start.4 = (bf16[16,64,1,8,72]{4,0,3,1,2:T(8,128)(2,1)S(1)}, bf16[16,64,1,8,72]{4,0,3,1,2:T(8,128)(2,1)}, u32[]{:S(2)}) copy-start(bf16[16,64,1,8,72]{4,0,3,1,2:T(8,128)(2,1)} %copy.23) | copy-start | bytes 3538948
